TPU v7x, 32 devices: a whole 2x2x4 slice. The times are simulated.
32 devices in a mesh: dp: 4 (over x, core), head: 8 (over z, y).
Axes of the slice: x: 2, y: 2, z: 4, core: 2. Of those that a mesh axis runs over, the one named last changes fastest.
Arguments:
- tokens: bfloat16 [24576, 1152], P(('dp', 'head')), may hold values from -6 to 6
- segment_ids: int32 [24576], P('dp'), may hold values from 0 to 95, as said below
- cond: float32 [96, 1152], P('dp'), may hold values from -6 to 6
- w_ada: bfloat16 [1152, 6912], P(None, 'head'), may hold values from -0.1875 to 0.1875
- b_ada: bfloat16 [6912], P('head'), may hold values from -4 to 4
- w_qkv: bfloat16 [1152, 3, 1152], P(None, None, 'head'), may hold values from -0.1875 to 0.1875
- bias_qv: bfloat16 [2, 1152], P(None, 'head'), may hold values from -4 to 4
- w_proj: bfloat16 [1152, 1152], P('head'), may hold values from -0.75 to 0.75
- b_proj: bfloat16 [1152], replicated, may hold values from -4 to 4
- w_fc1: bfloat16 [1152, 4608], P(None, 'head'), may hold values from -0.1875 to 0.1875
- b_fc1: bfloat16 [4608], P('head'), may hold values from -4 to 4
- w_fc2: bfloat16 [4608, 1152], P('head'), may hold values from -0.09375 to 0.09375
- b_fc2: bfloat16 [1152], replicated, may hold values from -4 to 4
- cotangent: bfloat16 [24576, 1152], P(('dp', 'head')), may hold values from -6 to 6
Outputs:
- out: bfloat16 [24576, 1152], P(('dp', 'head'))
- grad_tokens: bfloat16 [24576, 1152], P(('dp', 'head'))
- grad_cond: float32 [96, 1152], P('dp')
- grad_w_ada: float32 [1152, 6912], P(None, 'head')
- grad_b_ada: float32 [6912], P('head')
- grad_w_qkv: float32 [1152, 3, 1152], P(None, None, 'head')
- grad_bias_qv: float32 [2, 1152], P(None, 'head')
- grad_w_proj: float32 [1152, 1152], P('head')
- grad_b_proj: float32 [1152], replicated
- grad_w_fc1: float32 [1152, 4608], P(None, 'head')
- grad_b_fc1: float32 [4608], P('head')
- grad_w_fc2: float32 [4608, 1152], P('head')
- grad_b_fc2: float32 [1152], replicated
Inputs may be any that keep to these rules, and one draw needn't show every extreme that they name: `segment_ids`: each packed row of 2048 consecutive tokens is two halves of 1024 tokens, each either one segment or segments of 256 tokens. The ids of the tokens of index g of dp lie in g * 24 onward; a segment's id is that base plus (its first position within those tokens) // 256, so ids never fall and some slots name no token. In the last packed row of every index of dp the first half is one segment and the second half is split.
All inputs are finite; a program needn't handle non-finite values.
Results may differ from a plain program's by a relative error of at most 0.019.
The roundings to bfloat16 on the way count: a program that leaves them out, or rounds other values in their place, can miss the bound.
Values may be sent and summed in bfloat16 or wider, within the bound.
A program may use at most 320 MiB of HBM per device.

v0:
```python
import math
import jax
import jax.numpy as jnp
from jax import lax
from jax.sharding import PartitionSpec as P

HEAD_DIM = 72
PACK = 2048
norm_eps = 1e-06
top_precision = lax.Precision.HIGHEST


def layer_norm(values):
    centered = values - jnp.mean(values, axis=-1, keepdims=True)
    inverse = lax.rsqrt(jnp.mean(centered * centered, axis=-1, keepdims=True) + norm_eps)
    return (centered * inverse, inverse)


def norm_back(grad_normed, normed, inverse):
    mean_grad = jnp.mean(grad_normed, axis=-1, keepdims=True)
    mean_cross = jnp.mean(grad_normed * normed, axis=-1, keepdims=True)
    return inverse * (grad_normed - mean_grad - normed * mean_cross)


def gelu_tanh(values):
    return jax.nn.gelu(values, approximate=True)


def block_setup(query_row, key_row, value_row, head_width):
    length, columns = query_row.shape
    heads_here = columns // head_width
    block_rows = min(512, length)
    blocks = length // block_rows
    keys_split = key_row.reshape(length, heads_here, head_width)
    values_split = value_row.reshape(length, heads_here, head_width)
    queries_split = query_row.reshape(blocks, block_rows, heads_here, head_width)
    return (block_rows, blocks, keys_split, values_split, queries_split)


def row_forward(query_row, key_row, value_row, ident_row, head_width):
    block_rows, blocks, keys_split, values_split, queries_split = block_setup(
        query_row, key_row, value_row, head_width
    )
    scale = 1.0 / math.sqrt(head_width)
    ident_blocks = ident_row.reshape(blocks, block_rows)

    def one_block(inputs):
        query_block, ident_block = inputs
        scores = (
            jnp.einsum("qhd,khd->hqk", query_block, keys_split, preferred_element_type=jnp.float32)
            * scale
        )
        allowed = (ident_block[:, None] == ident_row[None, :])[None]
        scores = jnp.where(allowed, scores, -1e30)
        highest = jnp.max(scores, axis=-1, keepdims=True)
        weights = jnp.exp(scores - highest)
        totals = jnp.sum(weights, axis=-1, keepdims=True)
        probs = (weights / totals).astype(jnp.bfloat16)
        mixed = jnp.einsum("hqk,khd->qhd", probs, values_split, preferred_element_type=jnp.float32)
        return (
            mixed.reshape(block_rows, -1).astype(jnp.bfloat16),
            (highest + jnp.log(totals))[..., 0],
        )

    mixed, log_totals = lax.map(one_block, (queries_split, ident_blocks))
    return (mixed.reshape(query_row.shape), log_totals)


def row_backward(query_row, key_row, value_row, ident_row, log_row, grad_row, head_width):
    block_rows, blocks, keys_split, values_split, queries_split = block_setup(
        query_row, key_row, value_row, head_width
    )
    heads_here = keys_split.shape[1]
    scale = 1.0 / math.sqrt(head_width)
    grads_split = grad_row.reshape(blocks, block_rows, heads_here, head_width)
    ident_blocks = ident_row.reshape(blocks, block_rows)

    def one_block(carry, inputs):
        key_total, value_total = carry
        query_block, grad_block, ident_block, log_block = inputs
        scores = (
            jnp.einsum("qhd,khd->hqk", query_block, keys_split, preferred_element_type=jnp.float32)
            * scale
        )
        allowed = (ident_block[:, None] == ident_row[None, :])[None]
        probs = jnp.where(allowed, jnp.exp(scores - log_block[:, :, None]), 0.0)
        grad_probs = jnp.einsum(
            "qhd,khd->hqk", grad_block, values_split, preferred_element_type=jnp.float32
        )
        inner = jnp.sum(probs * grad_probs, axis=-1, keepdims=True)
        grad_scores = (probs * (grad_probs - inner)).astype(jnp.bfloat16)
        grad_query = (
            jnp.einsum("hqk,khd->qhd", grad_scores, keys_split, preferred_element_type=jnp.float32)
            * scale
        )
        key_total = (
            key_total
            + jnp.einsum(
                "hqk,qhd->khd", grad_scores, query_block, preferred_element_type=jnp.float32
            )
            * scale
        )
        value_total = value_total + jnp.einsum(
            "hqk,qhd->khd",
            probs.astype(jnp.bfloat16),
            grad_block,
            preferred_element_type=jnp.float32,
        )
        return ((key_total, value_total), grad_query.reshape(block_rows, -1).astype(jnp.bfloat16))

    zero_total = jnp.zeros(keys_split.shape, jnp.float32)
    (key_total, value_total), grad_query = lax.scan(
        one_block, (zero_total, zero_total), (queries_split, grads_split, ident_blocks, log_row)
    )
    length = ident_row.shape[0]
    return (
        grad_query.reshape(length, -1),
        key_total.reshape(length, -1).astype(jnp.bfloat16),
        value_total.reshape(length, -1).astype(jnp.bfloat16),
    )


def attend(query, keys, values, idents):
    packed = idents.shape[0] // PACK

    def one_row(inputs):
        return row_forward(inputs[0], inputs[1], inputs[2], inputs[3], HEAD_DIM)

    mixed, log_totals = lax.map(
        one_row,
        (
            query.reshape(packed, PACK, -1),
            keys.reshape(packed, PACK, -1),
            values.reshape(packed, PACK, -1),
            idents.reshape(packed, PACK),
        ),
    )
    return (mixed.reshape(query.shape), log_totals)


def attend_back(query, keys, values, idents, log_totals, grad_mix):
    packed = idents.shape[0] // PACK

    def one_row(inputs):
        return row_backward(
            inputs[0], inputs[1], inputs[2], inputs[3], inputs[4], inputs[5], HEAD_DIM
        )

    grad_query, grad_key, grad_value = lax.map(
        one_row,
        (
            query.reshape(packed, PACK, -1),
            keys.reshape(packed, PACK, -1),
            values.reshape(packed, PACK, -1),
            idents.reshape(packed, PACK),
            log_totals,
            grad_mix.reshape(packed, PACK, -1),
        ),
    )
    return (
        grad_query.reshape(query.shape),
        grad_key.reshape(query.shape),
        grad_value.reshape(query.shape),
    )


def local(
    tokens,
    segment_ids,
    cond,
    w_ada,
    b_ada,
    w_qkv,
    bias_qv,
    w_proj,
    b_proj,
    w_fc1,
    b_fc1,
    w_fc2,
    b_fc2,
    cotangent,
):
    rows_here, width = tokens.shape
    slots = cond.shape[0]
    columns = w_qkv.shape[2]
    row_start = lax.axis_index("head") * rows_here
    own_ids = (
        lax.dynamic_slice_in_dim(segment_ids, row_start, rows_here) - lax.axis_index("dp") * slots
    )
    pick = (own_ids[:, None] == jnp.arange(slots, dtype=jnp.int32)[None, :]).astype(jnp.float32)
    cond_act, silu_back = jax.vjp(jax.nn.silu, cond)
    cond_low = cond_act.astype(jnp.bfloat16)
    mod_part = jnp.dot(cond_low, w_ada, preferred_element_type=jnp.float32) + b_ada.astype(
        jnp.float32
    )
    modulation = lax.all_gather(mod_part, "head", axis=1, tiled=True)
    per_token = jnp.dot(pick, modulation, precision=top_precision)
    shift_a, scale_a, gate_a, shift_m, scale_m, gate_m = jnp.split(per_token, 6, axis=1)
    resid = tokens.astype(jnp.float32)
    normed_a, inverse_a = layer_norm(resid)
    attn_in = (normed_a * (1.0 + scale_a) + shift_a).astype(jnp.bfloat16)
    gathered_a = lax.all_gather(attn_in, "head", axis=0, tiled=True)
    qkv_weight = w_qkv.reshape(width, 3 * columns)
    qkv_bias = jnp.concatenate(
        [bias_qv[0], jnp.zeros((columns,), bias_qv.dtype), bias_qv[1]]
    ).astype(jnp.float32)
    qkv = (jnp.dot(gathered_a, qkv_weight, preferred_element_type=jnp.float32) + qkv_bias).astype(
        jnp.bfloat16
    )
    query = qkv[:, :columns]
    keys = qkv[:, columns : 2 * columns]
    values = qkv[:, 2 * columns :]
    attn_mix, log_totals = attend(query, keys, values, segment_ids)
    branch_a = lax.psum_scatter(
        jnp.dot(attn_mix, w_proj, preferred_element_type=jnp.float32),
        "head",
        scatter_dimension=0,
        tiled=True,
    ) + b_proj.astype(jnp.float32)
    mid = resid + gate_a * branch_a
    normed_m, inverse_m = layer_norm(mid)
    mlp_in = (normed_m * (1.0 + scale_m) + shift_m).astype(jnp.bfloat16)
    cotan = cotangent.astype(jnp.float32)
    grad_branch_m = (gate_m * cotan).astype(jnp.bfloat16)
    gathered_m = lax.all_gather(mlp_in, "head", axis=0, tiled=True)
    pre = jnp.dot(gathered_m, w_fc1, preferred_element_type=jnp.float32) + b_fc1.astype(jnp.float32)
    hidden, gelu_back = jax.vjp(gelu_tanh, pre)
    hidden_low = hidden.astype(jnp.bfloat16)
    branch_m = lax.psum_scatter(
        jnp.dot(hidden_low, w_fc2, preferred_element_type=jnp.float32).astype(jnp.bfloat16),
        "head",
        scatter_dimension=0,
        tiled=True,
    ).astype(jnp.float32) + b_fc2.astype(jnp.float32)
    grad_rows_m = lax.all_gather(grad_branch_m, "head", axis=0, tiled=True)
    grad_hidden = jnp.einsum("td,fd->tf", grad_rows_m, w_fc2, preferred_element_type=jnp.float32)
    grad_pre = gelu_back(grad_hidden)[0].astype(jnp.bfloat16)
    grad_fc1 = jnp.einsum("td,tf->df", gathered_m, grad_pre, preferred_element_type=jnp.float32)
    grad_fc2 = jnp.einsum("tf,td->fd", hidden_low, grad_rows_m, preferred_element_type=jnp.float32)
    grad_b1 = jnp.sum(grad_pre.astype(jnp.float32), axis=0)
    grad_mlp_in = lax.psum_scatter(
        jnp.einsum("tf,df->td", grad_pre, w_fc1, preferred_element_type=jnp.float32),
        "head",
        scatter_dimension=0,
        tiled=True,
    )
    output = (mid + gate_m * branch_m).astype(jnp.bfloat16)
    grad_mid = cotan + norm_back(grad_mlp_in * (1.0 + scale_m), normed_m, inverse_m)
    grad_branch_a = (gate_a * grad_mid).astype(jnp.bfloat16)
    grad_rows_a = lax.all_gather(grad_branch_a, "head", axis=0, tiled=True)
    grad_proj = jnp.einsum("tc,td->cd", attn_mix, grad_rows_a, preferred_element_type=jnp.float32)
    grad_mix = jnp.einsum(
        "td,cd->tc", grad_rows_a, w_proj, preferred_element_type=jnp.float32
    ).astype(jnp.bfloat16)
    grad_query, grad_key, grad_value = attend_back(
        query, keys, values, segment_ids, log_totals, grad_mix
    )
    grad_qkv = jnp.concatenate([grad_query, grad_key, grad_value], axis=1)
    grad_w_qkv = jnp.einsum(
        "td,tc->dc", gathered_a, grad_qkv, preferred_element_type=jnp.float32
    ).reshape(width, 3, columns)
    grad_bias_qv = jnp.stack(
        [
            jnp.sum(grad_query.astype(jnp.float32), axis=0),
            jnp.sum(grad_value.astype(jnp.float32), axis=0),
        ]
    )
    grad_attn_in = lax.psum_scatter(
        jnp.einsum("tc,dc->td", grad_qkv, qkv_weight, preferred_element_type=jnp.float32).astype(
            jnp.bfloat16
        ),
        "head",
        scatter_dimension=0,
        tiled=True,
    ).astype(jnp.float32)
    grad_tokens = (
        grad_mid + norm_back(grad_attn_in * (1.0 + scale_a), normed_a, inverse_a)
    ).astype(jnp.bfloat16)
    per_token_grad = jnp.concatenate(
        [
            grad_attn_in,
            grad_attn_in * normed_a,
            grad_mid * branch_a,
            grad_mlp_in,
            grad_mlp_in * normed_m,
            cotan * branch_m,
        ],
        axis=1,
    )
    grad_mod_part = jnp.einsum("ts,tm->sm", pick, per_token_grad, precision=top_precision)
    grad_mod = lax.psum_scatter(
        grad_mod_part.astype(jnp.bfloat16), "head", scatter_dimension=1, tiled=True
    ).astype(jnp.float32)
    grad_w_ada = jnp.einsum(
        "sd,sm->dm", cond_low.astype(jnp.float32), grad_mod, precision=top_precision
    )
    grad_b_ada = jnp.sum(grad_mod, axis=0)
    grad_cond_part = jnp.einsum(
        "sm,dm->sd", grad_mod, w_ada.astype(jnp.float32), precision=top_precision
    )
    proj_bias_part = jnp.sum(grad_branch_a.astype(jnp.float32), axis=0)
    mlp_bias_part = jnp.sum(grad_branch_m.astype(jnp.float32), axis=0)
    grad_cond_act, grad_b_proj, grad_b2 = (
        lax.psum(grad_cond_part.astype(jnp.bfloat16), "head").astype(jnp.float32),
        lax.psum(proj_bias_part.astype(jnp.bfloat16), "head").astype(jnp.float32),
        lax.psum(mlp_bias_part.astype(jnp.bfloat16), "head").astype(jnp.float32),
    )
    grad_cond = silu_back(grad_cond_act)[0]
    summed = (
        lax.psum(grad_w_ada.astype(jnp.bfloat16), "dp").astype(jnp.float32),
        lax.psum(grad_b_ada.astype(jnp.bfloat16), "dp").astype(jnp.float32),
        lax.psum(grad_w_qkv.astype(jnp.bfloat16), "dp").astype(jnp.float32),
        lax.psum(grad_bias_qv.astype(jnp.bfloat16), "dp").astype(jnp.float32),
        lax.psum(grad_proj.astype(jnp.bfloat16), "dp").astype(jnp.float32),
        lax.psum(grad_b_proj.astype(jnp.bfloat16), "dp").astype(jnp.float32),
        lax.psum(grad_fc1.astype(jnp.bfloat16), "dp").astype(jnp.float32),
        lax.psum(grad_b1.astype(jnp.bfloat16), "dp").astype(jnp.float32),
        lax.psum(grad_fc2.astype(jnp.bfloat16), "dp").astype(jnp.float32),
        lax.psum(grad_b2.astype(jnp.bfloat16), "dp").astype(jnp.float32),
    )
    return (output, grad_tokens, grad_cond) + tuple(summed)


def solution(mesh):
    placed = (
        P(("dp", "head"), None),
        P("dp"),
        P("dp", None),
        P(None, "head"),
        P("head"),
        P(None, None, "head"),
        P(None, "head"),
        P("head", None),
        P(),
        P(None, "head"),
        P("head"),
        P("head", None),
        P(),
        P(("dp", "head"), None),
    )
    return jax.shard_map(
        local,
        mesh=mesh,
        in_specs=placed,
        out_specs=(
            P(("dp", "head"), None),
            P(("dp", "head"), None),
            P("dp", None),
            P(None, "head"),
            P("head"),
            P(None, None, "head"),
            P(None, "head"),
            P("head", None),
            P(),
            P(None, "head"),
            P("head"),
            P("head", None),
            P(),
        ),
        check_vma=False,
    )
```

profile of v0, /device:TPU:0, one launch (start us, length us, event | category | flops | bytes accessed | tf_op | source)
XLA Modules:
  0.0 2927.3 jit_solution(12163566460413241053)
XLA Ops:
  12.7 33.5 %all-gather = f32[8,864,24]{1,2,0:T(8,128)S(1)} all-gather(f32[1,864,24]{1,2,0:T(8,128)S(1)} %fusion.64), channel_id=1, replica_groups=mesh['dp'=4,'head'=8] {'head'}, dimensions={0}, use_global_device_ids=true | all-gather | bytes 746496 | tf_op jit(solution)/shard_map/all_gather | solution.py:196
  46.7 8.6 fusion.66
  55.4 7.0 copy-done.3
  64.5 11.4 reduce-scatter.8.cloned.1.call-start
  76.1 184.8 %all-gather.6.cloned.1.call-done = bf16[6144,1152]{1,0:T(8,128)(2,1)} async-done(((bf16[768,1152]{1,0:T(8,128)(2,1)}), bf16[6144,1152]{1,0:T(8,128)(2,1)}) %all-gather.6.cloned.1.call-update) | async-done | bytes 14155792 | tf_op jit(solution)/shard_map/all_gather | solution.py:202
  260.9 10.3 add_convert_fusion
  277.1 140.8 %while.54 = (s32[]{:T(128)}, bf16[3,2048,144]{2,1,0:T(8,128)(2,1)}, f32[3,4,2,512]{3,2,1,0:T(2,128)}, bf16[3,2048,144]{1,2,0:T(8,128)(2,1)}, s32[3,2048]{1,0:T(4...) while((s32[]{:T(128)}, bf16[3,2048,144]{2,1,0:T(8,128)(2,1)}, ...), condition=%wide.region_7.8_spmd, body=%wide.region_2.7_spmd.sunk | while | flops 630266880 | bytes 39967056 | solution.py:129
  282.1 38.9 %while.57 = (s32[]{:T(128)}, bf16[4,512,144]{1,2,0:T(8,128)(2,1)}, f32[4,2,512]{2,1,0:T(2,128)S(1)}, s32[4,512]{1,0:T(4,128)S(1)}, s32[2048]{0:T(1024)S(1)}, /*i...) while((s32[]{:T(128)}, bf16[4,512,144]{1,2,0:T(8,128)(2,1)}, ...), condition=%wide.region_6.6_spmd, body=%wide.region_3.5_spmd.sunk | while | flops 630266880 | bytes 31176820 | solution.py:65
  329.0 38.9 %while.57 = (s32[]{:T(128)}, bf16[4,512,144]{1,2,0:T(8,128)(2,1)}, f32[4,2,512]{2,1,0:T(2,128)S(1)}, s32[4,512]{1,0:T(4,128)S(1)}, s32[2048]{0:T(1024)S(1)}, /*i...) while((s32[]{:T(128)}, bf16[4,512,144]{1,2,0:T(8,128)(2,1)}, ...), condition=%wide.region_6.6_spmd, body=%wide.region_3.5_spmd.sunk | while | flops 630266880 | bytes 31176820 | solution.py:65
  375.9 38.9 %while.57 = (s32[]{:T(128)}, bf16[4,512,144]{1,2,0:T(8,128)(2,1)}, f32[4,2,512]{2,1,0:T(2,128)S(1)}, s32[4,512]{1,0:T(4,128)S(1)}, s32[2048]{0:T(1024)S(1)}, /*i...) while((s32[]{:T(128)}, bf16[4,512,144]{1,2,0:T(8,128)(2,1)}, ...), condition=%wide.region_6.6_spmd, body=%wide.region_3.5_spmd.sunk | while | flops 630266880 | bytes 31176820 | solution.py:65
  417.8 15.5 fusion.85
  434.0 445.9 %reduce-scatter.8.cloned.1.call-done = f32[768,1152]{1,0:T(8,128)} async-done(((f32[6144,1152]{1,0:T(8,128)}), f32[768,1152]{1,0:T(8,128)}) %reduce-scatter.8.cloned.1.call-update) | async-done | bytes 3538960 | tf_op jit(solution)/shard_map/reduce_scatter | solution.py:214
  880.0 4.2 fusion.83
  886.0 5.1 fusion.62
  891.2 4.8 fusion.80
  896.0 189.6 %all-gather.8.cloned.1.call-done = bf16[6144,1152]{1,0:T(8,128)(2,1)} async-done(((bf16[768,1152]{1,0:T(8,128)(2,1)}), bf16[6144,1152]{1,0:T(8,128)(2,1)}) %all-gather.8.cloned.1.call-update) | async-done | bytes 14155792 | tf_op jit(solution)/shard_map/all_gather | solution.py:225
  1085.7 16.1 fusion.86
  1101.8 20.9 convolution_convert_fusion.1
  1122.8 159.0 %all-gather.10.cloned.1.call-done = bf16[6144,1152]{1,0:T(8,128)(2,1)} async-done(((bf16[768,1152]{1,0:T(8,128)(2,1)}), bf16[6144,1152]{1,0:T(8,128)(2,1)}) %all-gather.10.cloned.1.call-update) | async-done | bytes 14155792 | tf_op jit(solution)/shard_map/all_gather | solution.py:235
  1281.8 24.4 fusion.78
  1306.2 20.0 fusion.87
  1326.9 186.0 %reduce-scatter.10.cloned.1.call-done = bf16[768,1152]{1,0:T(8,128)(2,1)} async-done(((bf16[6144,1152]{1,0:T(8,128)(2,1)}), bf16[768,1152]{1,0:T(8,128)(2,1)}) %reduce-scatter.10.cloned.1.call-update) | async-done | bytes 1769488 | tf_op jit(solution)/shard_map/reduce_scatter | solution.py:229
  1512.9 451.3 %reduce-scatter.12.cloned.1.call-done = f32[768,1152]{1,0:T(8,128)} async-done(((f32[6144,1152]{1,0:T(8,128)}), f32[768,1152]{1,0:T(8,128)}) %reduce-scatter.12.cloned.1.call-update) | async-done | bytes 3538960 | tf_op jit(solution)/shard_map/reduce_scatter | solution.py:241
  1964.2 7.8 fusion.75
  1973.0 6.1 fusion.82
  1979.2 194.5 %all-gather.12.cloned.1.call-done = bf16[6144,1152]{1,0:T(8,128)(2,1)} async-done(((bf16[768,1152]{1,0:T(8,128)(2,1)}), bf16[6144,1152]{1,0:T(8,128)(2,1)}) %all-gather.12.cloned.1.call-update) | async-done | bytes 14155792 | tf_op jit(solution)/shard_map/all_gather | solution.py:250
  2173.6 9.7 convolution_convert_fusion.3
  2186.5 265.0 %while.56 = (s32[]{:T(128)}, bf16[3,2048,144]{2,1,0:T(8,128)(2,1)}, bf16[3,2048,144]{1,2,0:T(8,128)(2,1)}, bf16[3,2048,144]{1,2,0:T(8,128)(2,1)}, bf16[3,2048,14...) while((s32[]{:T(128)}, bf16[3,2048,144]{2,1,0:T(8,128)(2,1)}, ...), condition=%wide.region_19.20_spmd, body=%wide.region_15.19_spmd.sunk | while | flops 1544666112 | bytes 114133608 | solution.py:149
  2205.0 63.7 %while.58 = (s32[]{:T(128)}, f32[2048,2,72]{0,2,1:T(8,128)}, f32[2048,2,72]{0,2,1:T(8,128)}, bf16[4,512,144]{1,2,0:T(8,128)(2,1)}, bf16[4,512,2,72]{1,3,2,0:T(8,...) while((s32[]{:T(128)}, f32[2048,2,72]{0,2,1:T(8,128)}, ...), condition=%wide.region_18.18_spmd.clone, body=%wide.region_16.17_spmd.clone.sunk | while | flops 1544076288 | bytes 95906112 | solution.py:112
  2258.5 3.3 multiply_reduce_fusion.4
  2293.2 63.8 %while.58 = (s32[]{:T(128)}, f32[2048,2,72]{0,2,1:T(8,128)}, f32[2048,2,72]{0,2,1:T(8,128)}, bf16[4,512,144]{1,2,0:T(8,128)(2,1)}, bf16[4,512,2,72]{1,3,2,0:T(8,...) while((s32[]{:T(128)}, f32[2048,2,72]{0,2,1:T(8,128)}, ...), condition=%wide.region_18.18_spmd.clone, body=%wide.region_16.17_spmd.clone.sunk | while | flops 1544076288 | bytes 95906112 | solution.py:112
  2381.4 63.8 %while.58 = (s32[]{:T(128)}, f32[2048,2,72]{0,2,1:T(8,128)}, f32[2048,2,72]{0,2,1:T(8,128)}, bf16[4,512,144]{1,2,0:T(8,128)(2,1)}, bf16[4,512,2,72]{1,3,2,0:T(8,...) while((s32[]{:T(128)}, f32[2048,2,72]{0,2,1:T(8,128)}, ...), condition=%wide.region_18.18_spmd.clone, body=%wide.region_16.17_spmd.clone.sunk | while | flops 1544076288 | bytes 95906112 | solution.py:112
  2387.0 3.3 multiply_reduce_fusion.4
  2454.4 4.4 copy.92
  2461.8 11.1 convolution_convert_fusion
  2473.0 14.7 convolution_convert_fusion.5
  2487.8 20.8 convolution_convert_fusion.6
  2508.6 10.8 convolution_convert_fusion.7
  2519.4 181.3 %reduce-scatter.14.cloned.1.call-done = bf16[768,1152]{1,0:T(8,128)(2,1)} async-done(((bf16[6144,1152]{1,0:T(8,128)(2,1)}), bf16[768,1152]{1,0:T(8,128)(2,1)}) %reduce-scatter.14.cloned.1.call-update) | async-done | bytes 1769488 | tf_op jit(solution)/shard_map/reduce_scatter | solution.py:268
  2703.2 3.6 fusion.65
  2706.9 5.3 multiply_dynamic-update-slice_fusion.1
  2717.0 7.4 convolution_convert_fusion.2
  2726.0 9.3 convolution_convert_fusion.8
  2735.3 56.6 %reduce-scatter.16.cloned.1.call-done = bf16[864,24]{1,0:T(8,128)(2,1)} async-done(((bf16[6912,24]{1,0:T(8,128)(2,1)}), bf16[864,24]{1,0:T(8,128)(2,1)}) %reduce-scatter.16.cloned.1.call-update) | async-done | bytes 41488
  2800.0 35.5 %all-reduce = (bf16[24,1152]{1,0:T(8,128)(2,1)S(1)}, bf16[1152]{0:T(1024)(128)(2,1)S(1)}, bf16[1152]{0:T(1024)(128)(2,1)S(1)}) all-reduce(bf16[24,1152]{1,0:T(8,128)(2,1)S(1)} %convolution_convert_fusion.9, bf16[1152]{0:T(1024)(128)(2,1)S(1)} %copy-done.49, bf16[1152]{0:T(1024)(128)(2,1)S(1)} %copy-done.48), channel_id=1, replica_groups=mesh['dp'=4,'head'=8] {'head'}, use_global_device_ids=true, to_apply=%region_24.25 | all-reduce | flops 29952 | bytes 119808 | tf_op jit(solution)/shard_map/psum | solution.py:304
  2835.6 11.8 all-reduce.1
  2851.1 58.4 %all-reduce.5.cloned.1.call-done = (bf16[1152,864]{0,1:T(8,128)(2,1)}, bf16[1152,3,144]{0,2,1:T(8,128)(2,1)}, bf16[144,1152]{1,0:T(8,128)(2,1)}, bf16[1152,576]{0,1:T(8,128)(2,1)}, bf16[576,1152]{1,0:T(8,128)(2,1)}) async-done(((bf16[1152,864]{0,1:T(8,128)(2,1)}, bf16[1152,3,144]{0,2,1:T(8,128)(2,1)}, bf16[144,1152]{1,0:T(8,128)(2,1)}, bf16[1152,576]{0,1:T(8,128)(2,1)}, bf16[576,1152]{1,0:T(8,128)(2,1)}), ...) | async-done | bytes 5971984 | tf_op jit(solution)/shard_map/psum | solution.py:310
  2911.4 3.9 convert_element_type.244
  (604 shorter events, 451.6 us)
Async XLA Ops:
  7.2 4.8 copy-start
  7.2 4.8 copy-start.29
  7.2 253.7 %all-gather.6.cloned.1.call-start = ((), (), s32[]{:S(2)}) async-start(), calls=%async_computation.5 | async-start | bytes 15925248 | tf_op jit(solution)/shard_map/all_gather | solution.py:202
  9.9 45.5 %copy-start.37 = (f32[768]{0:T(1024)}, f32[768]{0:T(1024)S(1)}, u32[]{:S(2)}) copy-start(f32[768]{0:T(1024)S(1)} %broadcast_multiply_fusion.5) | copy-start | bytes 9220
  9.9 36.8 %copy-start.47 = (s32[6144]{0:T(1024)S(1)}, s32[6144]{0:T(1024)}, u32[]{:S(2)}) copy-start(s32[6144]{0:T(1024)} %param.23) | copy-start | bytes 73732
  12.0 43.4 %copy-start.45 = (f32[768]{0:T(1024)}, f32[768]{0:T(1024)S(1)}, u32[]{:S(2)}) copy-start(f32[768]{0:T(1024)S(1)} %add_rsqrt_fusion.1) | copy-start | bytes 9220
  46.7 8.7 copy-start.33
  46.7 15.7 copy-start.8
  55.4 7.1 copy-start.3
  62.4 13.5 copy-start.54
  62.4 198.5 %copy-start.58 = (bf16[1152,3,144]{0,2,1:T(8,128)(2,1)S(1)}, bf16[1152,3,144]{0,2,1:T(8,128)(2,1)}, u32[]{:S(2)}) copy-start(bf16[1152,3,144]{0,2,1:T(8,128)(2,1)} %param.27) | copy-start | bytes 2985988
  64.5 815.5 %reduce-scatter.8.cloned.1.call-start = ((), (), s32[]{:S(2)}) async-start(), calls=%async_computation.6 | async-start | bytes 31850496 | tf_op jit(solution)/shard_map/reduce_scatter | solution.py:214
  417.8 15.5 copy-start.31
  433.4 652.3 %all-gather.8.cloned.1.call-start = ((), (), s32[]{:S(2)}) async-start(), calls=%async_computation.7 | async-start | bytes 15925248 | tf_op jit(solution)/shard_map/all_gather | solution.py:225
  434.0 450.2 %copy-start.41 = (f32[1152]{0:T(1024)}, f32[1152]{0:T(1024)S(1)}, u32[]{:S(2)}) copy-start(f32[1152]{0:T(1024)S(1)} %convert_element_type.224) | copy-start | bytes 13828
  884.2 1087.7 %copy-start.35 = (f32[768]{0:T(1024)}, f32[768]{0:T(1024)S(1)}, u32[]{:S(2)}) copy-start(f32[768]{0:T(1024)S(1)} %broadcast_multiply_fusion.4) | copy-start | bytes 9220
  886.0 1085.9 %copy-start.39 = (f32[768]{0:T(1024)}, f32[768]{0:T(1024)S(1)}, u32[]{:S(2)}) copy-start(f32[768]{0:T(1024)S(1)} %add_rsqrt_fusion) | copy-start | bytes 9220
  891.1 4.9 copy-start.55
  891.1 390.6 %all-gather.10.cloned.1.call-start = ((), (), s32[]{:S(2)}) async-start(), calls=%async_computation.9 | async-start | bytes 15925248 | tf_op jit(solution)/shard_map/all_gather | solution.py:235
  896.0 616.9 %reduce-scatter.10.cloned.1.call-start = ((), (), s32[]{:S(2)}) async-start(), calls=%async_computation.8 | async-start | bytes 15925248 | tf_op jit(solution)/shard_map/reduce_scatter | solution.py:229
  896.0 385.7 %copy-start.52 = (f32[576]{0:T(1024)}, f32[576]{0:T(1024)S(1)}, u32[]{:S(2)}) copy-start(f32[576]{0:T(1024)S(1)} %convert_element_type.226) | copy-start | bytes 6916
  1085.7 16.1 copy-start.57
  1122.7 841.4 %reduce-scatter.12.cloned.1.call-start = ((), (), s32[]{:S(2)}) async-start(), calls=%async_computation.10 | async-start | bytes 31850496 | tf_op jit(solution)/shard_map/reduce_scatter | solution.py:241
  1326.2 847.4 %all-gather.12.cloned.1.call-start = ((), (), s32[]{:S(2)}) async-start(), calls=%async_computation.11 | async-start | bytes 15925248 | tf_op jit(solution)/shard_map/all_gather | solution.py:250
  1326.9 645.0 %copy-start.43 = (f32[1152]{0:T(1024)}, f32[1152]{0:T(1024)S(1)}, u32[]{:S(2)}) copy-start(f32[1152]{0:T(1024)S(1)} %convert_element_type.230) | copy-start | bytes 13828
  1964.1 7.8 copy-start.5
  1964.2 8.3 copy-start.10
  1964.2 8.8 copy-start.14
  1973.0 200.7 %copy-start.32 = (bf16[144,1152]{1,0:T(8,128)(2,1)S(1)}, bf16[144,1152]{1,0:T(8,128)(2,1)}, u32[]{:S(2)}) copy-start(bf16[144,1152]{1,0:T(8,128)(2,1)} %param.29) | copy-start | bytes 995332
  1979.1 721.6 %reduce-scatter.14.cloned.1.call-start = ((), (), s32[]{:S(2)}) async-start(), calls=%async_computation.12 | async-start | bytes 15925248 | tf_op jit(solution)/shard_map/reduce_scatter | solution.py:268
  2454.4 7.4 copy-start.59
  2472.9 14.8 copy-start.53
  2473.0 319.0 %reduce-scatter.16.cloned.1.call-start = ((), (), s32[]{:S(2)}) async-start(), calls=%async_computation.13 | async-start | bytes 1990656
  2487.8 20.8 copy-start.21
  2487.8 20.8 copy-start.23
  2487.8 20.8 copy-start.25
  2519.4 183.2 %copy-start.38 = (f32[768]{0:T(1024)S(1)}, f32[768]{0:T(1024)}, u32[]{:S(2)}) copy-start(f32[768]{0:T(1024)} %copy-done.37) | copy-start | bytes 9220
  2519.4 183.2 %copy-start.46 = (f32[768]{0:T(1024)S(1)}, f32[768]{0:T(1024)}, u32[]{:S(2)}) copy-start(f32[768]{0:T(1024)} %copy-done.45) | copy-start | bytes 9220
  2703.2 3.7 copy-start.42
  2706.9 5.4 copy-start.11
  2726.0 65.9 %copy-start.30 = (f32[24,1152]{1,0:T(8,128)S(1)}, f32[24,1152]{1,0:T(8,128)}, u32[]{:S(2)}) copy-start(f32[24,1152]{1,0:T(8,128)} %param.24) | copy-start | bytes 331780
  2726.0 183.5 %all-reduce.5.cloned.1.call-start = ((), (), s32[]{:S(2)}) async-start(), calls=%async_computation.14 | async-start | bytes 11943936 | tf_op jit(solution)/shard_map/psum | solution.py:310
  2794.8 4.7 copy-start.19
  2794.8 5.1 copy-start.48
  2794.9 5.1 copy-start.49
  2794.9 40.8 %copy-start.56 = (bf16[576]{0:T(1024)(128)(2,1)S(1)}, bf16[576]{0:T(1024)(128)(2,1)}, u32[]{:S(2)}) copy-start(bf16[576]{0:T(1024)(128)(2,1)} %get-tuple-element.468) | copy-start | bytes 3460
  2909.5 5.8 copy-start.28
  2911.4 5.3 copy-start.27
  (77 other events, 160.3 us)
Sparse Core Ops, SparseCore 0:
  64.6 196.2 all-gather.5
  433.5 446.4 reduce-scatter.7
  891.2 194.3 all-gather.7
  1088.3 193.4 all-gather.9
  1285.3 227.5 reduce-scatter.9
  1516.6 447.4 reduce-scatter.11
  1979.2 194.3 all-gather.11
  2473.1 227.5 reduce-scatter.13
  2726.1 65.7 reduce-scatter.15
  2795.6 113.8 all-reduce.4
where the time goes:
time: 2940 us; the launch traced here: 2930 us
  waiting for transfers between devices  2110 us (72%)
  matrix products  411 us (14%)
  other arithmetic  152 us (5%)
  local copies, waits for them, and re-layouts  147 us (5%)
  blocking collectives  80.8 us (3%)
    reduce_scatter x1, waiting for transfers between devices, local(): lax.psum_scatter(jnp.einsum('tf,df->td', grad_pre, w_fc1, preferred_eleme...  451 us
    reduce_scatter x1, waiting for transfers between devices, local(): lax.psum_scatter(jnp.dot(attn_mix, w_proj, preferred_element_type=jnp.flo...  446 us
    all_gather x1, waiting for transfers between devices, local(): grad_rows_a = lax.all_gather(grad_branch_a, 'head', axis=0, tiled=True)  194 us
    all_gather x1, waiting for transfers between devices, local(): gathered_m = lax.all_gather(mlp_in, 'head', axis=0, tiled=True)  190 us
    reduce_scatter x1, waiting for transfers between devices, local(): lax.psum_scatter(jnp.dot(hidden_low, w_fc2, preferred_element_type=jnp.fl...  186 us
    all_gather x1, waiting for transfers between devices, local(): gathered_a = lax.all_gather(attn_in, 'head', axis=0, tiled=True)  185 us
    reduce_scatter x1, waiting for transfers between devices, local(): lax.psum_scatter(jnp.einsum('tc,dc->td', grad_qkv, qkv_weight, preferred_...  181 us
    all_gather x1, waiting for transfers between devices, local(): grad_rows_m = lax.all_gather(grad_branch_m, 'head', axis=0, tiled=True)  159 us
  transfers between devices with their start and end apart: 10, of which 10 were waited for; matrix products, arithmetic and copies ran while one was open for 5% of the time, Pallas kernels for 0%

commit v1 on v0

--- a/solution.py
+++ b/solution.py
@@ -8,6 +8,19 @@
 PACK = 2048
 norm_eps = 1e-06
 top_precision = lax.Precision.HIGHEST
+
+
+def collect(x, axis, dim):
+    ways = lax.axis_size(axis)
+    up = [(d, (d + 1) % ways) for d in range(ways)]
+    down = [(d, (d - 1) % ways) for d in range(ways)]
+    earlier, later = ([x], [x])
+    for _ in range(ways // 2):
+        earlier.append(lax.ppermute(earlier[-1], axis, up))
+    for _ in range((ways - 1) // 2):
+        later.append(lax.ppermute(later[-1], axis, down))
+    line = jnp.concatenate([*earlier[::-1], *later[1:]], axis=dim)
+    return jnp.roll(line, (lax.axis_index(axis) - ways // 2) * x.shape[dim], axis=dim)
 
 
 def layer_norm(values):
@@ -247,7 +260,7 @@
     output = (mid + gate_m * branch_m).astype(jnp.bfloat16)
     grad_mid = cotan + norm_back(grad_mlp_in * (1.0 + scale_m), normed_m, inverse_m)
     grad_branch_a = (gate_a * grad_mid).astype(jnp.bfloat16)
-    grad_rows_a = lax.all_gather(grad_branch_a, "head", axis=0, tiled=True)
+    grad_rows_a = collect(grad_branch_a, "head", 0)
     grad_proj = jnp.einsum("tc,td->cd", attn_mix, grad_rows_a, preferred_element_type=jnp.float32)
     grad_mix = jnp.einsum(
         "td,cd->tc", grad_rows_a, w_proj, preferred_element_type=jnp.float32

time: 2940 us -> 3050 us (1.037)
  starting transfers between devices: 11.8 us -> 99.4 us
  local copies, waits for them, and re-layouts: 147 us -> 181 us
    all_gather x1 -> x0, waiting for transfers between devices: 194 us -> none  [local(): grad_rows_a = lax.all_gather(grad_branch_a, 'head', axis=0, tiled=True)]
    ppermute x0 -> x7, waiting for transfers between devices: none -> 186 us  [the longest x4 186 us: collect(): earlier.append(lax.ppermute(earlier[-1], axis, up))]
    ppermute x0 -> x7, starting transfers between devices: none -> 87.7 us  [the longest x3 81.1 us: collect(): later.append(lax.ppermute(later[-1], axis, down))]
    unnamed x113 -> x138, local copies, waits for them, and re-layouts: 18.1 us -> 50.6 us
  transfers between devices with their start and end apart: 10 -> 16, of which waited for: 10 -> 14; matrix products, arithmetic and copies ran while one was open for 5% -> 6% of each run, Pallas kernels for 0% -> 0%
where the time goes in v1:
time: 3050 us; the launch traced here: 3040 us
  waiting for transfers between devices  2100 us (69%)
  matrix products  414 us (14%)
  local copies, waits for them, and re-layouts  181 us (6%)
  other arithmetic  152 us (5%)
  starting transfers between devices  99.4 us (3%)
  blocking collectives  80.5 us (3%)
    reduce_scatter x1, waiting for transfers between devices, local(): lax.psum_scatter(jnp.einsum('tf,df->td', grad_pre, w_fc1, preferred_eleme...  451 us
    reduce_scatter x1, waiting for transfers between devices, local(): lax.psum_scatter(jnp.dot(attn_mix, w_proj, preferred_element_type=jnp.flo...  446 us
    reduce_scatter x1, waiting for transfers between devices, local(): lax.psum_scatter(jnp.einsum('tc,dc->td', grad_qkv, qkv_weight, preferred_...  193 us
    all_gather x1, waiting for transfers between devices, local(): gathered_m = lax.all_gather(mlp_in, 'head', axis=0, tiled=True)  190 us
    reduce_scatter x1, waiting for transfers between devices, local(): lax.psum_scatter(jnp.dot(hidden_low, w_fc2, preferred_element_type=jnp.fl...  188 us
    ppermute x4, waiting for transfers between devices, collect(): earlier.append(lax.ppermute(earlier[-1], axis, up))  186 us
    all_gather x1, waiting for transfers between devices, local(): gathered_a = lax.all_gather(attn_in, 'head', axis=0, tiled=True)  185 us
    all_gather x1, waiting for transfers between devices, local(): grad_rows_m = lax.all_gather(grad_branch_m, 'head', axis=0, tiled=True)  159 us
  transfers between devices with their start and end apart: 16, of which 14 were waited for; matrix products, arithmetic and copies ran while one was open for 6% of the time, Pallas kernels for 0%

profile of v1, /device:TPU:0, one launch (start us, length us, event | category | flops | bytes accessed | tf_op | source)
XLA Modules:
  0.0 3040.8 jit_solution(17746104285116108183)
XLA Ops:
  12.7 33.5 %all-gather = f32[8,864,24]{1,2,0:T(8,128)S(1)} all-gather(f32[1,864,24]{1,2,0:T(8,128)S(1)} %fusion.74), channel_id=1, replica_groups=mesh['dp'=4,'head'=8] {'head'}, dimensions={0}, use_global_device_ids=true | all-gather | bytes 746496 | tf_op jit(solution)/shard_map/all_gather | solution.py:209
  46.7 8.6 fusion.76
  55.4 7.0 copy-done.3
  64.5 11.4 reduce-scatter.8.cloned.1.call-start
  76.1 184.8 %all-gather.5.cloned.1.call-done = bf16[6144,1152]{1,0:T(8,128)(2,1)} async-done(((bf16[768,1152]{1,0:T(8,128)(2,1)}), bf16[6144,1152]{1,0:T(8,128)(2,1)}) %all-gather.5.cloned.1.call-update) | async-done | bytes 14155792 | tf_op jit(solution)/shard_map/all_gather | solution.py:215
  260.9 10.3 add_convert_fusion
  277.1 140.9 %while.54 = (s32[]{:T(128)}, bf16[3,2048,144]{2,1,0:T(8,128)(2,1)}, f32[3,4,2,512]{3,2,1,0:T(2,128)}, bf16[3,2048,144]{1,2,0:T(8,128)(2,1)}, s32[3,2048]{1,0:T(4...) while((s32[]{:T(128)}, bf16[3,2048,144]{2,1,0:T(8,128)(2,1)}, ...), condition=%wide.region_7.8_spmd, body=%wide.region_2.7_spmd.sunk | while | flops 630266880 | bytes 39967056 | solution.py:142
  282.1 38.9 %while.57 = (s32[]{:T(128)}, bf16[4,512,144]{1,2,0:T(8,128)(2,1)}, f32[4,2,512]{2,1,0:T(2,128)S(1)}, s32[4,512]{1,0:T(4,128)S(1)}, s32[2048]{0:T(1024)S(1)}, /*i...) while((s32[]{:T(128)}, bf16[4,512,144]{1,2,0:T(8,128)(2,1)}, ...), condition=%wide.region_6.6_spmd, body=%wide.region_3.5_spmd.sunk | while | flops 630266880 | bytes 31176820 | solution.py:78
  329.1 38.9 %while.57 = (s32[]{:T(128)}, bf16[4,512,144]{1,2,0:T(8,128)(2,1)}, f32[4,2,512]{2,1,0:T(2,128)S(1)}, s32[4,512]{1,0:T(4,128)S(1)}, s32[2048]{0:T(1024)S(1)}, /*i...) while((s32[]{:T(128)}, bf16[4,512,144]{1,2,0:T(8,128)(2,1)}, ...), condition=%wide.region_6.6_spmd, body=%wide.region_3.5_spmd.sunk | while | flops 630266880 | bytes 31176820 | solution.py:78
  376.1 38.9 %while.57 = (s32[]{:T(128)}, bf16[4,512,144]{1,2,0:T(8,128)(2,1)}, f32[4,2,512]{2,1,0:T(2,128)S(1)}, s32[4,512]{1,0:T(4,128)S(1)}, s32[2048]{0:T(1024)S(1)}, /*i...) while((s32[]{:T(128)}, bf16[4,512,144]{1,2,0:T(8,128)(2,1)}, ...), condition=%wide.region_6.6_spmd, body=%wide.region_3.5_spmd.sunk | while | flops 630266880 | bytes 31176820 | solution.py:78
  418.0 15.5 fusion.97
  434.2 446.0 %reduce-scatter.8.cloned.1.call-done = f32[768,1152]{1,0:T(8,128)} async-done(((f32[6144,1152]{1,0:T(8,128)}), f32[768,1152]{1,0:T(8,128)}) %reduce-scatter.8.cloned.1.call-update) | async-done | bytes 3538960 | tf_op jit(solution)/shard_map/reduce_scatter | solution.py:227
  886.2 5.1 fusion.69
  891.4 4.8 fusion.92
  896.2 189.6 %all-gather.7.cloned.1.call-done = bf16[6144,1152]{1,0:T(8,128)(2,1)} async-done(((bf16[768,1152]{1,0:T(8,128)(2,1)}), bf16[6144,1152]{1,0:T(8,128)(2,1)}) %all-gather.7.cloned.1.call-update) | async-done | bytes 14155792 | tf_op jit(solution)/shard_map/all_gather | solution.py:238
  1085.8 16.2 fusion.98
  1102.0 20.9 convolution_convert_fusion.1
  1123.0 158.9 %all-gather.9.cloned.1.call-done = bf16[6144,1152]{1,0:T(8,128)(2,1)} async-done(((bf16[768,1152]{1,0:T(8,128)(2,1)}), bf16[6144,1152]{1,0:T(8,128)(2,1)}) %all-gather.9.cloned.1.call-update) | async-done | bytes 14155792 | tf_op jit(solution)/shard_map/all_gather | solution.py:248
  1281.9 24.0 fusion.90
  1306.0 18.6 fusion.99
  1325.2 187.8 %reduce-scatter.10.cloned.1.call-done = bf16[768,1152]{1,0:T(8,128)(2,1)} async-done(((bf16[6144,1152]{1,0:T(8,128)(2,1)}), bf16[768,1152]{1,0:T(8,128)(2,1)}) %reduce-scatter.10.cloned.1.call-update) | async-done | bytes 1769488 | tf_op jit(solution)/shard_map/reduce_scatter | solution.py:242
  1513.0 451.3 %reduce-scatter.12.cloned.1.call-done = f32[768,1152]{1,0:T(8,128)} async-done(((f32[6144,1152]{1,0:T(8,128)}), f32[768,1152]{1,0:T(8,128)}) %reduce-scatter.12.cloned.1.call-update) | async-done | bytes 3538960 | tf_op jit(solution)/shard_map/reduce_scatter | solution.py:254
  1964.3 7.8 fusion.87
  1973.1 5.8 fusion.94
  1980.4 41.5 %collective-permute-done = bf16[768,1152]{1,0:T(8,128)(2,1)S(1)} collective-permute-done((bf16[768,1152]{1,0:T(8,128)(2,1)S(1)}, bf16[768,1152]{1,0:T(8,128)(2,1)S(1)}, u32[]{:S(2)}, u32[]{:S(2)}) %collective-permute-start) | collective-permute-done | bytes 1769504 | tf_op jit(solution)/shard_map/ppermute | solution.py:19
  2021.9 4.9 collective-permute-start.4
  2026.8 70.2 %collective-permute-done.1 = bf16[768,1152]{1,0:T(8,128)(2,1)S(1)} collective-permute-done((bf16[768,1152]{1,0:T(8,128)(2,1)S(1)}, bf16[768,1152]{1,0:T(8,128)(2,1)S(1)}, u32[]{:S(2)}, u32[]{:S(2)}) %collective-permute-start.1) | collective-permute-done | bytes 1769504 | tf_op jit(solution)/shard_map/ppermute | solution.py:19
  2099.6 37.5 %collective-permute-start.5 = (bf16[768,1152]{1,0:T(8,128)(2,1)}, bf16[768,1152]{1,0:T(8,128)(2,1)}, u32[]{:S(2)}, u32[]{:S(2)}) collective-permute-start(bf16[768,1152]{1,0:T(8,128)(2,1)} %collective-permute-done.4), channel_id=1, source_target_pairs={{0,7},{1,0},{2,1},{3,2},{4,3},{5,4},{6,5},{7,6},{8,15},{9,8},{10,9... | collective-permute-start | bytes 5308424 | tf_op jit(solution)/shard_map/ppermute | solution.py:21
  2137.1 37.6 %collective-permute-done.2 = bf16[768,1152]{1,0:T(8,128)(2,1)} collective-permute-done((bf16[768,1152]{1,0:T(8,128)(2,1)S(1)}, bf16[768,1152]{1,0:T(8,128)(2,1)}, u32[]{:S(2)}, u32[]{:S(2)}) %collective-permute-start.2) | collective-permute-done | bytes 1769504 | tf_op jit(solution)/shard_map/ppermute | solution.py:19
  2177.3 38.7 %collective-permute-start.6 = (bf16[768,1152]{1,0:T(8,128)(2,1)}, bf16[768,1152]{1,0:T(8,128)(2,1)S(1)}, u32[]{:S(2)}, u32[]{:S(2)}) collective-permute-start(bf16[768,1152]{1,0:T(8,128)(2,1)} %collective-permute-done.5), channel_id=1, source_target_pairs={{0,7},{1,0},{2,1},{3,2},{4,3},{5,4},{6,5},{7,6},{8,15},{9,8},{10,9... | collective-permute-start | bytes 5308424 | tf_op jit(solution)/shard_map/ppermute | solution.py:21
  2216.0 36.4 %collective-permute-done.3 = bf16[768,1152]{1,0:T(8,128)(2,1)} collective-permute-done((bf16[768,1152]{1,0:T(8,128)(2,1)}, bf16[768,1152]{1,0:T(8,128)(2,1)}, u32[]{:S(2)}, u32[]{:S(2)}) %collective-permute-start.3) | collective-permute-done | bytes 1769504 | tf_op jit(solution)/shard_map/ppermute | solution.py:19
  2286.3 9.9 fusion.50
  2299.4 265.4 %while.56 = (s32[]{:T(128)}, bf16[3,2048,144]{2,1,0:T(8,128)(2,1)}, bf16[3,2048,144]{1,2,0:T(8,128)(2,1)}, bf16[3,2048,144]{1,2,0:T(8,128)(2,1)}, bf16[3,2048,14...) while((s32[]{:T(128)}, bf16[3,2048,144]{2,1,0:T(8,128)(2,1)}, ...), condition=%wide.region_19.20_spmd, body=%wide.region_15.19_spmd.sunk | while | flops 1544666112 | bytes 114133608 | solution.py:162
  2318.0 63.9 %while.58 = (s32[]{:T(128)}, f32[2048,2,72]{0,2,1:T(8,128)}, f32[2048,2,72]{0,2,1:T(8,128)}, bf16[4,512,144]{1,2,0:T(8,128)(2,1)}, bf16[4,512,2,72]{1,3,2,0:T(8,...) while((s32[]{:T(128)}, f32[2048,2,72]{0,2,1:T(8,128)}, ...), condition=%wide.region_18.18_spmd.clone, body=%wide.region_16.17_spmd.clone.sunk | while | flops 1544076288 | bytes 95906112 | solution.py:125
  2406.2 63.9 %while.58 = (s32[]{:T(128)}, f32[2048,2,72]{0,2,1:T(8,128)}, f32[2048,2,72]{0,2,1:T(8,128)}, bf16[4,512,144]{1,2,0:T(8,128)(2,1)}, bf16[4,512,2,72]{1,3,2,0:T(8,...) while((s32[]{:T(128)}, f32[2048,2,72]{0,2,1:T(8,128)}, ...), condition=%wide.region_18.18_spmd.clone, body=%wide.region_16.17_spmd.clone.sunk | while | flops 1544076288 | bytes 95906112 | solution.py:125
  2494.5 63.9 %while.58 = (s32[]{:T(128)}, f32[2048,2,72]{0,2,1:T(8,128)}, f32[2048,2,72]{0,2,1:T(8,128)}, bf16[4,512,144]{1,2,0:T(8,128)(2,1)}, bf16[4,512,2,72]{1,3,2,0:T(8,...) while((s32[]{:T(128)}, f32[2048,2,72]{0,2,1:T(8,128)}, ...), condition=%wide.region_18.18_spmd.clone, body=%wide.region_16.17_spmd.clone.sunk | while | flops 1544076288 | bytes 95906112 | solution.py:125
  2575.1 11.0 convolution_convert_fusion
  2586.2 14.8 convolution_convert_fusion.4
  2601.0 20.6 convolution_convert_fusion.5
  2621.6 193.3 %reduce-scatter.14.cloned.1.call-done = bf16[768,1152]{1,0:T(8,128)(2,1)} async-done(((bf16[6144,1152]{1,0:T(8,128)(2,1)}), bf16[768,1152]{1,0:T(8,128)(2,1)}) %reduce-scatter.14.cloned.1.call-update) | async-done | bytes 1769488 | tf_op jit(solution)/shard_map/reduce_scatter | solution.py:281
  2821.2 5.3 multiply_dynamic-update-slice_fusion.1
  2831.2 7.4 convolution_convert_fusion.2
  2840.3 14.7 convolution_convert_fusion.6
  2855.0 10.4 fusion.71
  2865.4 40.8 %reduce-scatter.16.cloned.1.call-done = bf16[864,24]{1,0:T(8,128)(2,1)} async-done(((bf16[6912,24]{1,0:T(8,128)(2,1)}), bf16[864,24]{1,0:T(8,128)(2,1)}) %reduce-scatter.16.cloned.1.call-update) | async-done | bytes 41488
  2914.3 35.2 %all-reduce = (bf16[24,1152]{1,0:T(8,128)(2,1)S(1)}, bf16[1152]{0:T(1024)(128)(2,1)S(1)}, bf16[1152]{0:T(1024)(128)(2,1)S(1)}) all-reduce(bf16[24,1152]{1,0:T(8,128)(2,1)S(1)} %convolution_convert_fusion.7, bf16[1152]{0:T(1024)(128)(2,1)S(1)} %copy-done.53, bf16[1152]{0:T(1024)(128)(2,1)S(1)} %copy-done.52), channel_id=1, replica_groups=mesh['dp'=4,'head'=8] {'head'}, use_global_device_ids=true, to_apply=%region_24.25 | all-reduce | flops 29952 | bytes 119808 | tf_op jit(solution)/shard_map/psum | solution.py:317
  2949.6 11.8 all-reduce.1
  2965.1 58.3 %all-reduce.5.cloned.1.call-done = (bf16[1152,864]{0,1:T(8,128)(2,1)}, bf16[1152,3,144]{0,2,1:T(8,128)(2,1)}, bf16[144,1152]{1,0:T(8,128)(2,1)}, bf16[1152,576]{0,1:T(8,128)(2,1)}, bf16[576,1152]{1,0:T(8,128)(2,1)}) async-done(((bf16[1152,864]{0,1:T(8,128)(2,1)}, bf16[1152,3,144]{0,2,1:T(8,128)(2,1)}, bf16[144,1152]{1,0:T(8,128)(2,1)}, bf16[1152,576]{0,1:T(8,128)(2,1)}, bf16[576,1152]{1,0:T(8,128)(2,1)}), ...) | async-done | bytes 5971984 | tf_op jit(solution)/shard_map/psum | solution.py:323
  (641 shorter events, 515.4 us)
Async XLA Ops:
  7.2 253.7 %all-gather.5.cloned.1.call-start = ((), (), s32[]{:S(2)}) async-start(), calls=%async_computation.5 | async-start | bytes 15925248 | tf_op jit(solution)/shard_map/all_gather | solution.py:215
  9.9 45.5 %copy-start.41 = (f32[768]{0:T(1024)}, f32[768]{0:T(1024)S(1)}, u32[]{:S(2)}) copy-start(f32[768]{0:T(1024)S(1)} %broadcast_multiply_fusion.5) | copy-start | bytes 9220
  9.9 36.8 %copy-start.51 = (s32[6144]{0:T(1024)S(1)}, s32[6144]{0:T(1024)}, u32[]{:S(2)}) copy-start(s32[6144]{0:T(1024)} %param.23) | copy-start | bytes 73732
  12.0 43.4 %copy-start.49 = (f32[768]{0:T(1024)}, f32[768]{0:T(1024)S(1)}, u32[]{:S(2)}) copy-start(f32[768]{0:T(1024)S(1)} %add_rsqrt_fusion.1) | copy-start | bytes 9220
  46.7 8.7 copy-start.37
  46.7 15.7 copy-start.8
  55.4 7.0 copy-start.3
  62.4 13.5 copy-start.58
  62.4 198.5 %copy-start.63 = (bf16[1152,3,144]{0,2,1:T(8,128)(2,1)S(1)}, bf16[1152,3,144]{0,2,1:T(8,128)(2,1)}, u32[]{:S(2)}) copy-start(bf16[1152,3,144]{0,2,1:T(8,128)(2,1)} %param.27) | copy-start | bytes 2985988
  64.5 815.6 %reduce-scatter.8.cloned.1.call-start = ((), (), s32[]{:S(2)}) async-start(), calls=%async_computation.6 | async-start | bytes 31850496 | tf_op jit(solution)/shard_map/reduce_scatter | solution.py:227
  418.0 15.5 copy-start.35
  433.5 652.3 %all-gather.7.cloned.1.call-start = ((), (), s32[]{:S(2)}) async-start(), calls=%async_computation.7 | async-start | bytes 15925248 | tf_op jit(solution)/shard_map/all_gather | solution.py:238
  434.2 450.2 %copy-start.45 = (f32[1152]{0:T(1024)}, f32[1152]{0:T(1024)S(1)}, u32[]{:S(2)}) copy-start(f32[1152]{0:T(1024)S(1)} %convert_element_type.224) | copy-start | bytes 13828
  884.4 1087.7 %copy-start.39 = (f32[768]{0:T(1024)}, f32[768]{0:T(1024)S(1)}, u32[]{:S(2)}) copy-start(f32[768]{0:T(1024)S(1)} %broadcast_multiply_fusion.4) | copy-start | bytes 9220
  886.2 1085.9 %copy-start.43 = (f32[768]{0:T(1024)}, f32[768]{0:T(1024)S(1)}, u32[]{:S(2)}) copy-start(f32[768]{0:T(1024)S(1)} %add_rsqrt_fusion) | copy-start | bytes 9220
  891.3 390.6 %all-gather.9.cloned.1.call-start = ((), (), s32[]{:S(2)}) async-start(), calls=%async_computation.9 | async-start | bytes 15925248 | tf_op jit(solution)/shard_map/all_gather | solution.py:248
  896.2 616.9 %reduce-scatter.10.cloned.1.call-start = ((), (), s32[]{:S(2)}) async-start(), calls=%async_computation.8 | async-start | bytes 15925248 | tf_op jit(solution)/shard_map/reduce_scatter | solution.py:242
  896.2 385.7 %copy-start.56 = (f32[576]{0:T(1024)}, f32[576]{0:T(1024)S(1)}, u32[]{:S(2)}) copy-start(f32[576]{0:T(1024)S(1)} %convert_element_type.226) | copy-start | bytes 6916
  896.2 205.8 %copy-start.61 = (bf16[576,1152]{1,0:T(8,128)(2,1)S(1)}, bf16[576,1152]{1,0:T(8,128)(2,1)}, u32[]{:S(2)}) copy-start(bf16[576,1152]{1,0:T(8,128)(2,1)} %param.33) | copy-start | bytes 3981316
  1123.0 841.3 %reduce-scatter.12.cloned.1.call-start = ((), (), s32[]{:S(2)}) async-start(), calls=%async_computation.10 | async-start | bytes 31850496 | tf_op jit(solution)/shard_map/reduce_scatter | solution.py:254
  1281.9 24.0 copy-start.62
  1324.6 1490.4 %reduce-scatter.14.cloned.1.call-start = ((), (), s32[]{:S(2)}) async-start(), calls=%async_computation.11 | async-start | bytes 15925248 | tf_op jit(solution)/shard_map/reduce_scatter | solution.py:281
  1325.2 646.8 %copy-start.47 = (f32[1152]{0:T(1024)}, f32[1152]{0:T(1024)S(1)}, u32[]{:S(2)}) copy-start(f32[1152]{0:T(1024)S(1)} %convert_element_type.230) | copy-start | bytes 13828
  1964.3 7.8 copy-start.5
  1964.3 8.3 copy-start.10
  1964.3 8.8 copy-start.15
  1978.9 43.0 %copy-start.17 = (bf16[768,1152]{1,0:T(8,128)(2,1)}, bf16[768,1152]{1,0:T(8,128)(2,1)S(1)}, u32[]{:S(2)}) copy-start(bf16[768,1152]{1,0:T(8,128)(2,1)S(1)} %get-tuple-element.473) | copy-start | bytes 5308420
  1978.9 43.0 %collective-permute-start = (bf16[768,1152]{1,0:T(8,128)(2,1)S(1)}, bf16[768,1152]{1,0:T(8,128)(2,1)S(1)}, u32[]{:S(2)}, u32[]{:S(2)}) collective-permute-start(bf16[768,1152]{1,0:T(8,128)(2,1)S(1)} %get-tuple-element.473), channel_id=1, source_target_pairs={{0,1},{1,2},{2,3},{3,4},{4,5},{5,6},{6,7},{7,0},{8,9},{9,10},{10,1... | collective-permute-start | bytes 5308424 | tf_op jit(solution)/shard_map/ppermute | solution.py:19
  2021.9 77.7 %copy-start.22 = (bf16[768,1152]{1,0:T(8,128)(2,1)}, bf16[768,1152]{1,0:T(8,128)(2,1)S(1)}, u32[]{:S(2)}) copy-start(bf16[768,1152]{1,0:T(8,128)(2,1)S(1)} %collective-permute-done) | copy-start | bytes 5308420
  2021.9 75.1 %collective-permute-start.1 = (bf16[768,1152]{1,0:T(8,128)(2,1)S(1)}, bf16[768,1152]{1,0:T(8,128)(2,1)S(1)}, u32[]{:S(2)}, u32[]{:S(2)}) collective-permute-start(bf16[768,1152]{1,0:T(8,128)(2,1)S(1)} %collective-permute-done), channel_id=1, source_target_pairs={{0,1},{1,2},{2,3},{3,4},{4,5},{5,6},{6,7},{7,0},{8,9},{9,10},{10,1... | collective-permute-start | bytes 5308424 | tf_op jit(solution)/shard_map/ppermute | solution.py:19
  2021.9 77.7 %collective-permute-start.4 = (bf16[768,1152]{1,0:T(8,128)(2,1)S(1)}, bf16[768,1152]{1,0:T(8,128)(2,1)}, u32[]{:S(2)}, u32[]{:S(2)}) collective-permute-start(bf16[768,1152]{1,0:T(8,128)(2,1)S(1)} %get-tuple-element.473), channel_id=1, source_target_pairs={{0,7},{1,0},{2,1},{3,2},{4,3},{5,4},{6,5},{7,6},{8,15},{9,8},{10,9... | collective-permute-start | bytes 5308424 | tf_op jit(solution)/shard_map/ppermute | solution.py:21
  2097.0 40.1 %copy-start.24 = (bf16[768,1152]{1,0:T(8,128)(2,1)}, bf16[768,1152]{1,0:T(8,128)(2,1)S(1)}, u32[]{:S(2)}) copy-start(bf16[768,1152]{1,0:T(8,128)(2,1)S(1)} %collective-permute-done.1) | copy-start | bytes 5308420
  2097.0 77.7 %collective-permute-start.2 = (bf16[768,1152]{1,0:T(8,128)(2,1)S(1)}, bf16[768,1152]{1,0:T(8,128)(2,1)}, u32[]{:S(2)}, u32[]{:S(2)}) collective-permute-start(bf16[768,1152]{1,0:T(8,128)(2,1)S(1)} %collective-permute-done.1), channel_id=1, source_target_pairs={{0,1},{1,2},{2,3},{3,4},{4,5},{5,6},{6,7},{7,0},{8,9},{9,10},{10,1... | collective-permute-start | bytes 5308424 | tf_op jit(solution)/shard_map/ppermute | solution.py:19
  2099.6 77.7 %collective-permute-start.5 = (bf16[768,1152]{1,0:T(8,128)(2,1)}, bf16[768,1152]{1,0:T(8,128)(2,1)}, u32[]{:S(2)}, u32[]{:S(2)}) collective-permute-start(bf16[768,1152]{1,0:T(8,128)(2,1)} %collective-permute-done.4), channel_id=1, source_target_pairs={{0,7},{1,0},{2,1},{3,2},{4,3},{5,4},{6,5},{7,6},{8,15},{9,8},{10,9... | collective-permute-start | bytes 5308424 | tf_op jit(solution)/shard_map/ppermute | solution.py:21
  2174.7 77.7 %collective-permute-start.3 = (bf16[768,1152]{1,0:T(8,128)(2,1)}, bf16[768,1152]{1,0:T(8,128)(2,1)}, u32[]{:S(2)}, u32[]{:S(2)}) collective-permute-start(bf16[768,1152]{1,0:T(8,128)(2,1)} %collective-permute-done.2), channel_id=1, source_target_pairs={{0,1},{1,2},{2,3},{3,4},{4,5},{5,6},{6,7},{7,0},{8,9},{9,10},{10,1... | collective-permute-start | bytes 5308424 | tf_op jit(solution)/shard_map/ppermute | solution.py:19
  2177.3 80.9 %copy-start.25 = (bf16[768,1152]{1,0:T(8,128)(2,1)S(1)}, bf16[768,1152]{1,0:T(8,128)(2,1)}, u32[]{:S(2)}) copy-start(bf16[768,1152]{1,0:T(8,128)(2,1)} %copy-done.24) | copy-start | bytes 5308420
  2177.3 90.7 %collective-permute-start.6 = (bf16[768,1152]{1,0:T(8,128)(2,1)}, bf16[768,1152]{1,0:T(8,128)(2,1)S(1)}, u32[]{:S(2)}, u32[]{:S(2)}) collective-permute-start(bf16[768,1152]{1,0:T(8,128)(2,1)} %collective-permute-done.5), channel_id=1, source_target_pairs={{0,7},{1,0},{2,1},{3,2},{4,3},{5,4},{6,5},{7,6},{8,15},{9,8},{10,9... | collective-permute-start | bytes 5308424 | tf_op jit(solution)/shard_map/ppermute | solution.py:21
  2567.7 7.4 copy-start.64
  2586.2 14.8 copy-start.57
  2586.2 320.0 %reduce-scatter.16.cloned.1.call-start = ((), (), s32[]{:S(2)}) async-start(), calls=%async_computation.12 | async-start | bytes 1990656
  2621.6 195.2 %copy-start.42 = (f32[768]{0:T(1024)S(1)}, f32[768]{0:T(1024)}, u32[]{:S(2)}) copy-start(f32[768]{0:T(1024)} %copy-done.41) | copy-start | bytes 9220
  2621.6 195.2 %copy-start.50 = (f32[768]{0:T(1024)S(1)}, f32[768]{0:T(1024)}, u32[]{:S(2)}) copy-start(f32[768]{0:T(1024)} %copy-done.49) | copy-start | bytes 9220
  2821.2 5.3 copy-start.11
  2840.2 183.1 %all-reduce.5.cloned.1.call-start = ((), (), s32[]{:S(2)}) async-start(), calls=%async_computation.13 | async-start | bytes 11943936 | tf_op jit(solution)/shard_map/psum | solution.py:323
  2840.3 14.7 copy-start.14
  2855.0 51.2 %copy-start.34 = (f32[24,1152]{1,0:T(8,128)S(1)}, f32[24,1152]{1,0:T(8,128)}, u32[]{:S(2)}) copy-start(f32[24,1152]{1,0:T(8,128)} %param.24) | copy-start | bytes 331780
  2909.2 40.5 %copy-start.60 = (bf16[576]{0:T(1024)(128)(2,1)S(1)}, bf16[576]{0:T(1024)(128)(2,1)}, u32[]{:S(2)}) copy-start(bf16[576]{0:T(1024)(128)(2,1)} %get-tuple-element.468) | copy-start | bytes 3460
  3023.3 5.8 copy-start.32
  (88 other events, 210.4 us)
Sparse Core Ops, SparseCore 0:
  64.6 196.2 all-gather.4
  433.6 446.4 reduce-scatter.7
  891.4 194.3 all-gather.6
  1088.4 193.4 all-gather.8
  1285.4 227.5 reduce-scatter.9
  1516.8 447.4 reduce-scatter.11
  2586.3 228.6 reduce-scatter.13
  2840.4 65.7 reduce-scatter.15
  2909.5 113.7 all-reduce.4
